TPU v7x, 32 devices: a whole 2x2x4 slice. The times are simulated.
32 devices in a mesh: section: 4 (over x, core), tp: 8 (over z, y).
Axes of the slice: x: 2, y: 2, z: 4, core: 2. Of those that a mesh axis runs over, the one named last changes fastest.
Arguments:
- pending_activation: bfloat16 [4, 128, 4096], P('section'), may hold values from -6 to 6
- admissible_microbatches: bfloat16 [4, 128, 4096], P(None, None, 'tp'), may hold values from -6 to 6
- arrival_plan: int32 [4], replicated, may hold values from 0 to 3, each once
- vanished_hop: int32 [1], replicated, may hold values from 1 to 3
- query_key_value_matrices: bfloat16 [4, 4096, 3, 2048], P('section', None, None, 'tp')
- mixing_projection_matrices: bfloat16 [4, 2048, 4096], P('section', 'tp'), may hold values from -0.125 to 0.125
- normalizer_factors: bfloat16 [4, 4096], P('section'), may hold values from 0.25 to 1.75
Outputs:
- activation_later: bfloat16 [4, 128, 4096], P('section')
- standby_input: bfloat16 [4, 128, 4096], P('section', None, 'tp')
Inputs may be any that keep to these rules, and one draw needn't show every extreme that they name: `vanished_hop`: the preempted section is not the first. `arrival_plan`: each micro-batch index once.
All inputs are finite; a program needn't handle non-finite values.
Results may differ from a plain program's by a relative error of at most 0.013.
Values may be sent and summed in bfloat16 or wider, within the bound.
A program may use at most 64 MiB of HBM per device.

v0:
```python
import functools

import jax
import jax.numpy as jnp
from jax import lax
from jax.experimental import pallas as pl
from jax.experimental.pallas import tpu as pltpu
from jax.sharding import PartitionSpec as P

HD = 128
TICKS = 3
NORM_EPS = 1e-05
MESH = pl.DeviceIdType.MESH
PIECES = 4


def relay_kernel(
    sections, nz, ny,
    lost_ref, plan_ref, pend_ref, pool_ref, win_hbm, wout_hbm, gain_ref,
    later_ref, standby_ref,
    win_ref, wout_ref, w_sem, x_buf, y_buf, acc, qkv, ctx, part, own_part, ry_buf, zs_buf, rz_buf, fwd_buf, last_buf, spare_in,
    ag_zs, ag_zr, ag_ys, ag_yr, rs_zs, rs_zr, rs_ys, rs_yr, sh_s, sh_r,
):
    steps = TICKS + 2
    s = lax.axis_index("section")
    me = lax.axis_index("tp")
    z, y = me // ny, me % ny
    nxt, prv = (s + 1) % sections, (s + sections - 1) % sections
    lost = lost_ref[0]
    devices = nz * ny
    rows, width = x_buf.shape[2], x_buf.shape[3]
    cols = wout_ref.shape[0]
    heads = cols // HD

    def partner(at, mask):
        bit = 1
        while bit <= mask:
            if mask & bit:
                at = at + bit - 2 * bit * ((at // bit) % 2)
            bit *= 2
        return at

    def tp_at(dz, dy):
        return partner(z, dz) * ny + partner(y, dy)

    win_copy = pltpu.make_async_copy(win_hbm, win_ref, w_sem.at[0])
    wout_copy = pltpu.make_async_copy(wout_hbm, wout_ref, w_sem.at[1])
    win_copy.start()
    wout_copy.start()
    barrier = pltpu.get_barrier_semaphore()
    for dz in range(1, nz):
        pl.semaphore_signal(barrier, inc=1, device_id={"section": s, "tp": tp_at(dz, 0)}, device_id_type=MESH)
    for dy in range(1, ny):
        pl.semaphore_signal(barrier, inc=1, device_id={"section": s, "tp": tp_at(0, dy)}, device_id_type=MESH)
    pl.semaphore_signal(barrier, inc=1, device_id={"section": nxt, "tp": me}, device_id_type=MESH)
    pl.semaphore_signal(barrier, inc=1, device_id={"section": prv, "tp": me}, device_id_type=MESH)
    pl.semaphore_wait(barrier, nz + ny)

    def copy_to(src, dst, send, recv, section, tp):
        return pltpu.make_async_remote_copy(
            src_ref=src, dst_ref=dst, send_sem=send, recv_sem=recv,
            device_id={"section": section, "tp": tp}, device_id_type=MESH,
        )

    def span(h):
        return pl.ds(h * (rows // PIECES), rows // PIECES)

    def block_copy(n, slot, h, send, recv, tp):
        return copy_to(x_buf.at[n, slot, span(h)], x_buf.at[n, slot, span(h)], send, recv, s, tp)

    def z_copy(n, h, dz, slot):
        return block_copy(n, slot, h, ag_zs.at[h, dz], ag_zr.at[n, h, dz], tp_at(dz, 0))

    def y_copy(n, h, dz, dy, slot):
        return block_copy(n, slot, h, ag_ys.at[h, dz, dy], ag_yr.at[n, h, dz, dy], tp_at(0, dy))

    def ag_start(n):
        for dz in range(1, nz):
            for h in range(PIECES):
                z_copy(n, h, dz, me).start()
        for dy in range(1, ny):
            for h in range(PIECES):
                y_copy(n, h, 0, dy, me).start()

    def ag_forward(n):
        for dz in range(1, nz):
            for h in range(PIECES):
                z_copy(n, h, dz, tp_at(dz, 0)).wait_recv()
                for dy in range(1, ny):
                    y_copy(n, h, dz, dy, tp_at(dz, 0)).start()

    def ag_finish(n):
        for h in range(PIECES):
            for dz in range(nz):
                for dy in range(1, ny):
                    y_copy(n, h, dz, dy, tp_at(dz, dy)).wait_recv()
            for dz in range(1, nz):
                z_copy(n, h, dz, me).wait_send()
            for dz in range(nz):
                for dy in range(1, ny):
                    y_copy(n, h, dz, dy, tp_at(dz, 0)).wait_send()

    def layer(n):
        def add_sum(j, total):
            return total + jnp.sum(x_buf[n, j].astype(jnp.float32), axis=-1, keepdims=True)

        count = float(devices * width)
        mean = lax.fori_loop(0, devices, add_sum, jnp.zeros((rows, 1), jnp.float32)) / count

        def add_square(j, total):
            centered = x_buf[n, j].astype(jnp.float32) - mean
            return total + jnp.sum(centered * centered, axis=-1, keepdims=True)

        var = lax.fori_loop(0, devices, add_square, jnp.zeros((rows, 1), jnp.float32)) / count
        rstd = lax.rsqrt(var + NORM_EPS)

        @pl.when(n == 0)
        def _():
            win_copy.wait()
            wout_copy.wait()

        acc[...] = jnp.zeros_like(acc)

        def project(j, carry):
            at = pl.ds(pl.multiple_of(j * width, 128), width)
            gain = gain_ref[:, at].astype(jnp.float32)
            normed = ((x_buf[n, j].astype(jnp.float32) - mean) * rstd * gain).astype(jnp.bfloat16)
            for i in range(3):
                acc[:, i * cols:(i + 1) * cols] += jnp.dot(
                    normed, win_ref[i, at, :], preferred_element_type=jnp.float32
                )
            return carry

        lax.fori_loop(0, devices, project, 0)
        qkv[...] = acc[...].astype(jnp.bfloat16)
        causal = lax.broadcasted_iota(jnp.int32, (rows, rows), 0) >= lax.broadcasted_iota(jnp.int32, (rows, rows), 1)
        for h in range(heads):
            q = qkv[:, h * HD:(h + 1) * HD]
            k = qkv[:, cols + h * HD:cols + (h + 1) * HD]
            v = qkv[:, 2 * cols + h * HD:2 * cols + (h + 1) * HD]
            scores = lax.dot_general(q, k, (((1,), (1,)), ((), ())), preferred_element_type=jnp.float32)
            scores = jnp.where(causal, scores * HD ** (-0.5), -jnp.inf)
            weights = jnp.exp(scores - jnp.max(scores, axis=-1, keepdims=True))
            probs = (weights / jnp.sum(weights, axis=-1, keepdims=True)).astype(jnp.bfloat16)
            ctx[:, h * HD:(h + 1) * HD] = jnp.dot(probs, v, preferred_element_type=jnp.float32).astype(jnp.bfloat16)

        def partial_for(tp):
            at = pl.ds(pl.multiple_of(tp * width, 128), width)
            return jnp.dot(ctx[...], wout_ref[:, at], preferred_element_type=jnp.float32)

        order = list(range(nz - 1, -1, -1))
        sends, got = [], {}
        for dz in order:
            for dy in range(1, ny):
                part[dy - 1, dz] = partial_for(tp_at(dz, dy)).astype(jnp.bfloat16)
                for h in range(PIECES):
                    got[dz, dy, h] = copy_to(part.at[dy - 1, dz, span(h)], ry_buf.at[n, dy - 1, dz, span(h)],
                                             rs_ys.at[h, dz, dy], rs_yr.at[n, h, dz, dy], s, tp_at(0, dy))
                    got[dz, dy, h].start()
        for dz in order:
            own_part[dz] = partial_for(tp_at(dz, 0))
        for dz in order:
            for h in range(PIECES):
                total = own_part[dz, span(h)]
                for dy in range(1, ny):
                    got[dz, dy, h].wait_recv()
                    total = total + ry_buf[n, dy - 1, dz, span(h)].astype(jnp.float32)
                if dz:
                    zs_buf[dz - 1, span(h)] = total.astype(jnp.bfloat16)
                    sends.append(copy_to(zs_buf.at[dz - 1, span(h)], rz_buf.at[n, dz - 1, span(h)],
                                         rs_zs.at[h, dz], rs_zr.at[n, h, dz], s, tp_at(dz, 0)))
                    sends[-1].start()
                else:
                    own_part[0, span(h)] = total

        @pl.when((s == 0) & (n < TICKS - 1))
        def _():
            ag_forward(n + 1)

        @pl.when(n == TICKS + 1)
        def _():
            ag_forward(steps)

        total = own_part[0]
        for copy in sends:
            copy.wait_recv()
        for dz in range(1, nz):
            total = total + rz_buf[n, dz - 1].astype(jnp.float32)
        y_buf[n] = (x_buf[n, me].astype(jnp.float32) + total).astype(jnp.bfloat16)
        for copy in list(got.values()) + sends:
            copy.wait_send()

    def needed(section, n):
        tail = (n <= TICKS) | (section > 2) | (section == 0)
        live = (section + TICKS - 1 >= n) | ((section == 0) & (n == TICKS + 1))
        if sections <= TICKS + 1:
            live = live & ((section != sections - 1) | (n != TICKS - 1))
        return live & tail

    def passes(section, n):
        return needed(section, n) & (n > 0) & ((section > 0) | (n == TICKS + 1))

    def shift_copy(n):
        return copy_to(fwd_buf, x_buf.at[n, me], sh_s.at[0], sh_r.at[n], nxt, me)

    def pick(cond, a, b):
        return jnp.where(jnp.full(a.shape, cond), a, b)

    def own_rows():
        settled = pick((s < lost) | (s - TICKS + 1 > lost), y_buf[TICKS - 1], y_buf[TICKS])
        return pick(s == lost, y_buf[0], settled)

    out_copy = copy_to(last_buf.at[0], x_buf.at[steps, me], sh_s.at[1], sh_r.at[steps], nxt, me)

    def step(n, carry):
        @pl.when(needed(s, n))
        def _():
            @pl.when(n == 0)
            def _():
                for j in range(devices):
                    rows_j = pend_ref[0, :, j * width:(j + 1) * width]
                    x_buf[0, j] = pick(s == lost, jnp.zeros_like(rows_j), rows_j)

            @pl.when(passes(s, n))
            def _():
                shift_copy(n).wait_recv()
                ag_start(n)
                ag_forward(n)

            @pl.when(n > 0)
            def _():
                ag_finish(n)

            @pl.when((s == 0) & (n < TICKS - 1))
            def _():
                x_buf[n + 1, me] = pool_ref[plan_ref[n]]
                ag_start(n + 1)

            @pl.when(n == TICKS + 1)
            def _():
                out_copy.wait_recv()
                ag_start(steps)

            layer(n)

        @pl.when(jnp.logical_not(needed(s, n)))
        def _():
            y_buf[n] = jnp.zeros((rows, width), jnp.bfloat16)

            @pl.when(n == TICKS + 1)
            def _():
                out_copy.wait_recv()
                ag_start(steps)
                ag_forward(steps)

        @pl.when((n < steps - 1) & passes(nxt, n + 1))
        def _():
            fwd_buf[...] = y_buf[n]

            @pl.when((n == TICKS) & (s == sections - 1))
            def _():
                fwd_buf[...] = own_rows()

            copy = shift_copy(n + 1)
            copy.start()
            copy.wait_send()

        @pl.when(n == TICKS)
        def _():
            final = pick(s == lost, y_buf[TICKS], own_rows())
            final = pick(nxt == 0, pool_ref[plan_ref[TICKS - 1]], final)
            last_buf[0] = pick(nxt == lost, jnp.zeros_like(final), final)
            out_copy.start()

        return carry

    lax.fori_loop(0, steps, step, 0)

    settled = pick((s - 1 < lost) | (s - TICKS > lost), y_buf[TICKS], y_buf[TICKS + 1])
    spare = pick(s - 1 == lost, y_buf[1], settled)
    spare = pick(s == 0, y_buf[TICKS + 1], spare)
    last_buf[1] = spare
    spare_copy = copy_to(last_buf.at[1], spare_in, sh_s.at[0], sh_r.at[0], nxt, me)
    spare_copy.start()
    ag_finish(steps)
    for j in range(devices):
        later_ref[0, :, j * width:(j + 1) * width] = x_buf[steps, j]
    spare_copy.wait_recv()
    standby_ref[0] = spare_in[...]
    out_copy.wait_send()
    spare_copy.wait_send()


def solution(mesh):
    sections, devices = mesh.shape["section"], mesh.shape["tp"]
    ny = 1
    while (2 * ny) * (2 * ny) <= devices and devices % (2 * ny) == 0:
        ny *= 2
    nz = devices // ny

    def per_device(pend, pool, plan, lost, win, wout, gain):
        rows, hidden = pend.shape[1], pend.shape[2]
        width = hidden // devices
        cols = win.shape[3]
        slots = TICKS + 3
        win = jnp.transpose(win[0], (1, 0, 2))
        vmem = pl.BlockSpec(memory_space=pltpu.VMEM)
        smem = pl.BlockSpec(memory_space=pltpu.SMEM)
        hbm = pl.BlockSpec(memory_space=pl.ANY)
        bf = functools.partial(pltpu.VMEM, dtype=jnp.bfloat16)
        dma = pltpu.SemaphoreType.DMA
        return pl.pallas_call(
            functools.partial(relay_kernel, sections, nz, ny),
            out_shape=(
                jax.ShapeDtypeStruct((1, rows, hidden), jnp.bfloat16),
                jax.ShapeDtypeStruct((1, rows, width), jnp.bfloat16),
            ),
            in_specs=[smem, smem, vmem, vmem, hbm, hbm, vmem],
            out_specs=(vmem, vmem),
            scratch_shapes=[
                bf((3, hidden, cols)),
                bf((cols, hidden)),
                dma((2,)),
                bf((slots, devices, rows, width)),
                bf((slots, rows, width)),
                pltpu.VMEM((rows, 3 * cols), jnp.float32),
                bf((rows, 3 * cols)),
                bf((rows, cols)),
                bf((ny - 1, nz, rows, width)),
                pltpu.VMEM((nz, rows, width), jnp.float32),
                bf((slots, ny - 1, nz, rows, width)),
                bf((nz - 1, rows, width)),
                bf((slots, nz - 1, rows, width)),
                bf((rows, width)),
                bf((2, rows, width)),
                bf((rows, width)),
                dma((PIECES, nz)), dma((slots, PIECES, nz)), dma((PIECES, nz, ny)), dma((slots, PIECES, nz, ny)),
                dma((PIECES, nz)), dma((slots, PIECES, nz)), dma((PIECES, nz, ny)), dma((slots, PIECES, nz, ny)),
                dma((2,)), dma((slots,)),
            ],
            compiler_params=pltpu.CompilerParams(
                collective_id=0, has_side_effects=True, vmem_limit_bytes=60 * 1024 * 1024
            ),
        )(lost, plan, pend, pool, win, wout[0], gain)

    placed = (
        P("section", None, None),
        P(None, None, "tp"),
        P(),
        P(),
        P("section", None, None, "tp"),
        P("section", "tp", None),
        P("section", None),
    )
    return jax.shard_map(
        per_device,
        mesh=mesh,
        in_specs=placed,
        out_specs=(P("section", None, None), P("section", None, "tp")),
        check_vma=False,
    )
```

profile of v0, /device:TPU:0, one launch (start us, length us, event | category | flops | bytes accessed | tf_op | source)
XLA Modules:
  0.0 172.9 jit_solution(5038142936994487237)
XLA Ops:
  1.3 167.8 %shard_map.86 = (bf16[1,128,4096]{2,1,0:T(8,128)(2,1)}, bf16[1,128,512]{2,1,0:T(8,128)(2,1)}) custom-call(s32[1]{0:T(128)S(6)} %copy.11.lost_ref, s32[4]{0:T(128)} %plan_ref.1, bf16[1,128,4096]{2,1,0:T(8,128)(2,1)} %pend_ref.1, bf16[4,128,512]{2,1,0:T(8,128)(2,1)} %pool_ref.1, bf16[3,4096,256]{2,1,0:T(8,128)(2,1)} %bitcast.4, bf16[256,4096]{1,0:T(8,128)(2,1)} %bitcast.5, ...), custom_call_target="tpu_custom_call" | custom-call | tf_op jit(solution)/shard_map/pallas_call | solution.py:312
  169.0 2.3 %copy.12 = bf16[1,128,4096]{2,1,0:T(8,128)(2,1)} copy(bf16[1,128,4096]{2,1,0:T(8,128)(2,1)} %get-tuple-element.4) | data formatting | bytes 2097152
  171.3 1.6 copy.13
where the time goes:
time: 173 us
  Pallas kernels  168 us (97%)
  local copies, waits for them, and re-layouts  3.85 us (2%)
    pallas_call x1, Pallas kernels, per_device(): pl.pallas_call(functools.partial(relay_kernel, sections, nz, ny), out_sha...  168 us
    unnamed x2, local copies, waits for them, and re-layouts  3.85 us

commit v1 on v0

v1 whole, which is shorter than its diff:
```python
import functools

import jax
import jax.numpy as jnp
from jax import lax
from jax.experimental import pallas as pl
from jax.experimental.pallas import tpu as pltpu
from jax.sharding import PartitionSpec as P

HD = 128
TICKS = 3
NORM_EPS = 1e-05
MESH = pl.DeviceIdType.MESH
PIECES = 4
HALVES = 2
LANES = 128


def relay_kernel(
    sections, nz, ny,
    lost_ref, plan_ref, pend_hbm, pool_hbm, win_hbm, wout_hbm, gain_ref,
    later_hbm, standby_hbm,
    win_ref, wout_ref, pool_buf, x_buf, y_buf, pivot, sum_1, sum_2, csum, acc, qkv, ctx,
    part, own_part, ry_buf, zs_buf, rz_buf, fwd_buf, spare_buf, spare_in,
    w_sem, x_sem, io_sem, fw_s, ag_zs, ag_zr, ag_ys, ag_yr, rs_zs, rs_zr, rs_ys, rs_yr, sp_s, sp_r,
):
    steps = TICKS + 2
    s = lax.axis_index("section")
    me = lax.axis_index("tp")
    z, y = me // ny, me % ny
    nxt, prv = (s + 1) % sections, (s + sections - 1) % sections
    lost = lost_ref[0]
    devices = nz * ny
    rows, width = x_buf.shape[2], x_buf.shape[3]
    cols = wout_ref.shape[0]
    heads = cols // HD
    half = rows // HALVES
    per_half = PIECES // HALVES
    count = float(devices * width)
    far = list(range(nz - 1, -1, -1))

    def partner(at, mask):
        bit = 1
        while bit <= mask:
            if mask & bit:
                at = at + bit - 2 * bit * ((at // bit) % 2)
            bit *= 2
        return at

    def tp_at(dz, dy):
        return partner(z, dz) * ny + partner(y, dy)

    def columns(j):
        return pl.ds(pl.multiple_of(j * width, LANES), width)

    def win_copy(j):
        return pltpu.make_async_copy(win_hbm.at[:, columns(j), :], win_ref.at[:, columns(j), :], w_sem.at[j])

    def pend_copy(j):
        return pltpu.make_async_copy(pend_hbm.at[0, :, columns(j)], x_buf.at[0, j], x_sem.at[j])

    wout_copy = pltpu.make_async_copy(wout_hbm, wout_ref, io_sem.at[0])
    pool_copy = pltpu.make_async_copy(pool_hbm, pool_buf, io_sem.at[1])
    pool_copy.start()
    for j in range(devices):
        pend_copy(j).start()
        win_copy(j).start()
    wout_copy.start()

    barrier = pltpu.get_barrier_semaphore()
    for dz in range(nz):
        if dz:
            pl.semaphore_signal(barrier, inc=1, device_id={"section": s, "tp": tp_at(dz, 0)}, device_id_type=MESH)
        pl.semaphore_signal(barrier, inc=1, device_id={"section": nxt, "tp": tp_at(dz, 0)}, device_id_type=MESH)
        pl.semaphore_signal(barrier, inc=1, device_id={"section": prv, "tp": tp_at(dz, 0)}, device_id_type=MESH)
    for dy in range(1, ny):
        pl.semaphore_signal(barrier, inc=1, device_id={"section": s, "tp": tp_at(0, dy)}, device_id_type=MESH)
    pl.semaphore_wait(barrier, 3 * nz + ny - 2)

    def copy_to(src, dst, send, recv, section, tp):
        return pltpu.make_async_remote_copy(
            src_ref=src, dst_ref=dst, send_sem=send, recv_sem=recv,
            device_id={"section": section, "tp": tp}, device_id_type=MESH,
        )

    def span(h):
        return pl.ds(h * (rows // PIECES), rows // PIECES)

    def pick(cond, a, b):
        return jnp.where(jnp.full(a.shape, cond), a, b)

    def needed(section, n):
        tail = (n <= TICKS) | (section > 2) | (section == 0)
        live = (section + TICKS - 1 >= n) | ((section == 0) & (n == TICKS + 1))
        if sections <= TICKS + 1:
            live = live & ((section != sections - 1) | (n != TICKS - 1))
        return live & tail

    def passes(section, n):
        layered = needed(section, n) & (n > 0) & ((section > 0) | (n == TICKS + 1))
        return layered | ((section > 1) & (n == TICKS + 1))

    def pooled(n):
        return (s == 0) & (((n > 0) & (n < TICKS)) | (n == steps))

    def small(n):
        return (n < s) if sections <= TICKS + 1 else (n < 0)

    def when_full(n, h, body):
        if h == 0:
            body()
        else:
            pl.when(jnp.logical_not(small(n)))(body)

    def z_copy(n, h, dz, slot):
        block = x_buf.at[n, slot, span(h)]
        return copy_to(block, block, ag_zs.at[n - 1], ag_zr.at[n - 1, h, dz], s, tp_at(dz, 0))

    def y_copy(n, h, dz, dy, slot):
        block = x_buf.at[n, slot, span(h)]
        return copy_to(block, block, ag_ys.at[n - 1], ag_yr.at[n - 1, h, dz, dy - 1], s, tp_at(0, dy))

    def fwd_copy(n, h, dz):
        return copy_to(
            fwd_buf.at[n, span(h)], x_buf.at[n + 1, me, span(h)],
            fw_s.at[n], ag_zr.at[n, h, dz], nxt, tp_at(dz, 0),
        )

    def spare_copy(h):
        return copy_to(spare_buf.at[span(h)], spare_in.at[span(h)], sp_s.at[0], sp_r.at[h], nxt, me)

    def sent(ref, sem):
        copy_to(ref, ref, sem, sp_r.at[0], nxt, me).wait_send()

    def sent_blocks(n, blocks, sem):
        @pl.when(jnp.logical_not(small(n)))
        def _():
            sent(x_buf.at[n, pl.ds(0, blocks)], sem)

        if sections <= TICKS + 1:
            @pl.when(small(n))
            def _():
                sent(x_buf.at[n, pl.ds(0, blocks), span(0)], sem)

    def later_copy(j):
        return pltpu.make_async_copy(x_buf.at[steps, j], later_hbm.at[0, :, columns(j)], x_sem.at[j])

    def pool_start(n, tick):
        x_buf[n, me] = pool_buf[plan_ref[tick]]
        for h in range(PIECES):
            for dz in far[:-1]:
                z_copy(n, h, dz, me).start()
            for dy in range(1, ny):
                y_copy(n, h, 0, dy, me).start()

    def forward(n, h, first):
        for dz in range(first, nz):
            z_copy(n, h, dz, tp_at(dz, 0)).wait_recv()
            for dy in range(1, ny):
                y_copy(n, h, dz, dy, tp_at(dz, 0)).start()

    def pool_forward(n):
        for h in range(PIECES):
            forward(n, h, 1)

    def forward_all(n, pieces):
        for h in pieces:
            when_full(n, h, functools.partial(forward, n, h, 0))

    def arrive(n, h, dz):
        for dy in range(1, ny):
            y_copy(n, h, dz, dy, tp_at(dz, dy)).wait_recv()

    def arrive_all(n):
        for h in range(PIECES):
            for dz in range(nz):
                arrive(n, h, dz)

    def blank(n):
        if sections <= TICKS + 1:
            @pl.when(small(n))
            def _():
                deep = rows // PIECES
                for j in range(devices):
                    x_buf[n, j, deep:] = jnp.zeros((rows - deep, width), jnp.bfloat16)

    def tally(xf, at, base):
        s_1 = jnp.zeros((xf.shape[0], LANES), jnp.float32)
        s_2 = jnp.zeros((xf.shape[0], LANES), jnp.float32)
        for c in range(width // LANES):
            d = xf[:, c * LANES:(c + 1) * LANES] - base
            s_1 = s_1 + d
            s_2 = s_2 + d * d
        sum_1[at] += s_1
        sum_2[at] += s_2

    def open_rows(xf, at):
        shape = (xf.shape[0], LANES)
        pivot[at] = jnp.broadcast_to(jnp.sum(xf, axis=-1, keepdims=True) * (1.0 / width), shape)
        sum_1[at] = jnp.zeros(shape, jnp.float32)
        sum_2[at] = jnp.zeros(shape, jnp.float32)

    every = pl.ds(0, rows)

    def first_rows(j, carry):
        pend_copy(j).wait()
        rows_j = x_buf[0, j]
        rows_j = pick((s == lost) | small(0), jnp.zeros_like(rows_j), rows_j)
        x_buf[0, j] = rows_j
        xf = rows_j.astype(jnp.float32)

        @pl.when(j == 0)
        def _():
            open_rows(xf, every)
            acc[...] = jnp.zeros_like(acc)
            csum[...] = jnp.zeros_like(csum)

        tally(xf, every, pivot[...])
        gain = jnp.broadcast_to(gain_ref[:, columns(j)].astype(jnp.float32), (LANES, width)).T
        gain = jnp.concatenate([gain] * (cols // LANES), axis=1)
        ones = jnp.ones((8, width), jnp.bfloat16)
        win_copy(j).wait()
        for i in range(3):
            scaled = (win_ref[i, columns(j), :].astype(jnp.float32) * gain).astype(jnp.bfloat16)
            win_ref[i, columns(j), :] = scaled
            at = slice(i * cols, (i + 1) * cols)
            csum[:, at] += jnp.dot(ones, scaled, preferred_element_type=jnp.float32)
            acc[:, at] += jnp.dot(rows_j, scaled, preferred_element_type=jnp.float32)
        return carry

    def unit(n, r, dz, dy):
        j = tp_at(dz, dy)
        at = pl.ds(r * half, half)
        block = x_buf[n, j, at]
        xf = block.astype(jnp.float32)
        if dz == 0 and dy == 0:
            open_rows(xf, at)
        tally(xf, at, pivot[at])
        for i in range(3):
            product = jnp.dot(block, win_ref[i, columns(j), :], preferred_element_type=jnp.float32)
            if dz == 0 and dy == 0:
                acc[at, i * cols:(i + 1) * cols] = product
            else:
                acc[at, i * cols:(i + 1) * cols] += product

    def gather_project(n):
        handed = passes(s, n)

        def take(r):
            @pl.when(handed)
            def _():
                forward_all(n, range(r * per_half, (r + 1) * per_half))

        def near(r):
            for dz in range(nz):
                unit(n, r, dz, 0)

        def across(r):
            for dz in range(nz):
                for h in range(r * per_half, (r + 1) * per_half):
                    when_full(n, h, functools.partial(arrive, n, h, dz))
                for dy in range(1, ny):
                    unit(n, r, dz, dy)

        blank(n)
        take(0)
        near(0)
        for r in range(1, HALVES):
            take(r)
            across(r - 1)
            near(r)
        across(HALVES - 1)

    def attend():
        m = jnp.sum(sum_1[...], axis=-1, keepdims=True) * (1.0 / count)
        var = jnp.maximum(jnp.sum(sum_2[...], axis=-1, keepdims=True) * (1.0 / count) - m * m, 0.0)
        mean = pivot[:, 0:1] + m
        rstd = lax.rsqrt(var + NORM_EPS)
        qkv[...] = ((acc[...] - mean * csum[0:1, :]) * rstd).astype(jnp.bfloat16)
        causal = lax.broadcasted_iota(jnp.int32, (rows, rows), 0) >= lax.broadcasted_iota(jnp.int32, (rows, rows), 1)
        for h in range(heads):
            q = qkv[:, h * HD:(h + 1) * HD]
            k = qkv[:, cols + h * HD:cols + (h + 1) * HD]
            v = qkv[:, 2 * cols + h * HD:2 * cols + (h + 1) * HD]
            scores = lax.dot_general(q, k, (((1,), (1,)), ((), ())), preferred_element_type=jnp.float32)
            scores = jnp.where(causal, scores * HD ** (-0.5), -jnp.inf)
            weights = jnp.exp(scores - jnp.max(scores, axis=-1, keepdims=True))
            probs = (weights / jnp.sum(weights, axis=-1, keepdims=True)).astype(jnp.bfloat16)
            ctx[:, h * HD:(h + 1) * HD] = jnp.dot(probs, v, preferred_element_type=jnp.float32).astype(jnp.bfloat16)

    def settled(section, h):
        early = (section < lost) | (section - TICKS + 1 > lost)
        return pick(early, y_buf[TICKS - 1, span(h)], y_buf[TICKS, span(h)])

    def send_spare(h):
        early = (s - 1 < lost) | (s - TICKS > lost)
        spare = pick(early, y_buf[TICKS, span(h)], y_buf[TICKS + 1, span(h)])
        spare = pick(s - 1 == lost, y_buf[1, span(h)], spare)
        spare_buf[span(h)] = pick(s == 0, y_buf[TICKS + 1, span(h)], spare)
        spare_copy(h).start()

    def write_later():
        @pl.when(s == 1)
        def _():
            for j in range(devices):
                rows_j = x_buf[TICKS, j]
                x_buf[steps, j] = pick(s == lost, jnp.zeros_like(rows_j), rows_j)

        @pl.when(s > 1)
        def _():
            behind = s - 1
            early = (behind != lost) & ((behind < lost) | (behind - TICKS + 1 > lost))
            for j in range(devices):
                rows_j = pick(early, x_buf[TICKS, j], x_buf[TICKS + 1, j])
                x_buf[steps, j] = pick(s == lost, jnp.zeros_like(rows_j), rows_j)

        @pl.when(s > 0)
        def _():
            for j in range(devices):
                later_copy(j).start()

    def project_out(n):
        def partial_for(tp):
            return jnp.dot(ctx[...], wout_ref[:, columns(tp)], preferred_element_type=jnp.float32)

        turn = n % 3
        def crossed(dy, h):
            return copy_to(part.at[dy - 1, :, span(h)], ry_buf.at[turn, dy - 1, :, span(h)],
                           rs_ys.at[0], rs_yr.at[turn, h, dy - 1], s, tp_at(0, dy))

        def summed(dz, h):
            return copy_to(zs_buf.at[dz - 1, span(h)], rz_buf.at[turn, dz - 1, span(h)],
                           rs_zs.at[0], rs_zr.at[turn, h, dz - 1], s, tp_at(dz, 0))

        def cross(h):
            for dy in range(1, ny):
                crossed(dy, h).start()

        for dz in far:
            for dy in range(1, ny):
                part[dy - 1, dz] = partial_for(tp_at(dz, dy)).astype(jnp.bfloat16)
        for h in range(PIECES):
            when_full(n, h, functools.partial(cross, h))

        @pl.when((s == 0) & (n == 0))
        def _():
            pool_forward(1)

        for dz in far:
            own_part[dz] = partial_for(tp_at(dz, 0))

        @pl.when(n == TICKS + 1)
        def _():
            write_later()

        def over_y(h):
            for dy in range(1, ny):
                crossed(dy, h).wait_recv()
            for dz in far:
                total = own_part[dz, span(h)]
                for dy in range(1, ny):
                    total = total + ry_buf[turn, dy - 1, dz, span(h)].astype(jnp.float32)
                if dz:
                    zs_buf[dz - 1, span(h)] = total.astype(jnp.bfloat16)
                    summed(dz, h).start()
                else:
                    own_part[0, span(h)] = total

        def over_z(h):
            total = own_part[0, span(h)]
            for dz in range(1, nz):
                summed(dz, h).wait_recv()
                total = total + rz_buf[turn, dz - 1, span(h)].astype(jnp.float32)
            y_buf[n, span(h)] = (x_buf[n, me, span(h)].astype(jnp.float32) + total).astype(jnp.bfloat16)

            @pl.when((n < steps - 1) & passes(nxt, n + 1))
            def _():
                fwd_buf[n, span(h)] = y_buf[n, span(h)]

                @pl.when((n == TICKS) & (s == sections - 1))
                def _():
                    fwd_buf[n, span(h)] = pick(s == lost, y_buf[0, span(h)], settled(s, h))

                for dz in far:
                    fwd_copy(n, h, dz).start()

            @pl.when(n == TICKS + 1)
            def _():
                send_spare(h)

        for h in range(PIECES):
            when_full(n, h, functools.partial(over_y, h))
            if h == PIECES - 2:
                over_z(0)
        for h in range(1, PIECES):
            when_full(n, h, functools.partial(over_z, h))

        @pl.when(jnp.logical_not(small(n)))
        def _():
            sent(part, rs_ys.at[0])
            sent(zs_buf, rs_zs.at[0])

        if sections <= TICKS + 1:
            @pl.when(small(n))
            def _():
                for h in range(1, PIECES):
                    y_buf[n, span(h)] = y_buf[n, span(0)]
                sent(part.at[:, :, span(0)], rs_ys.at[0])
                sent(zs_buf.at[:, span(0)], rs_zs.at[0])

    def step(n, carry):
        @pl.when(needed(s, n))
        def _():
            @pl.when(n == 0)
            def _():
                @pl.when(s == 0)
                def _():
                    pool_copy.wait()
                    pool_start(1, 0)

                lax.fori_loop(0, devices, first_rows, 0)
                wout_copy.wait()

            @pl.when(n > 0)
            def _():
                gather_project(n)

            attend()
            project_out(n)

            @pl.when((s == 0) & (n == 1))
            def _():
                pool_start(2, 1)
                pool_forward(2)

        @pl.when(jnp.logical_not(needed(s, n)))
        def _():
            y_buf[n] = jnp.zeros((rows, width), jnp.bfloat16)

            @pl.when((s == 0) & (n == TICKS))
            def _():
                pool_start(steps, TICKS - 1)
                pool_forward(steps)
                arrive_all(steps)
                for j in range(devices):
                    later_copy(j).start()

            @pl.when(n == TICKS + 1)
            def _():
                for h in range(PIECES):
                    send_spare(h)

                @pl.when(passes(s, n))
                def _():
                    forward_all(n, range(PIECES))
                    arrive_all(n)

                write_later()

        return carry

    @pl.when(s > 0)
    def _():
        pool_copy.wait()

    lax.fori_loop(0, steps, step, 0)

    def drain(n, carry):
        @pl.when(passes(nxt, n) & (n < steps))
        def _():
            sent_blocks(n - 1, nz, fw_s.at[n - 1])

        @pl.when(pooled(n))
        def _():
            sent(x_buf.at[n, pl.ds(0, nz - 1)], ag_zs.at[n - 1])

        @pl.when(pooled(n) | (passes(s, n) & (n < steps)))
        def _():
            sent_blocks(n, nz * (ny - 1), ag_ys.at[n - 1])

        return carry

    def standby_copy(h):
        return pltpu.make_async_copy(spare_in.at[span(h)], standby_hbm.at[0, span(h), :], w_sem.at[h])

    for h in range(PIECES):
        spare_copy(h).wait_recv()
        standby_copy(h).start()
    lax.fori_loop(1, steps + 1, drain, 0)
    for j in range(devices):
        later_copy(j).wait()
    sent(spare_buf, sp_s.at[0])
    for h in range(PIECES):
        standby_copy(h).wait()


def solution(mesh):
    sections, devices = mesh.shape["section"], mesh.shape["tp"]
    ny = 1
    while (2 * ny) * (2 * ny) <= devices and devices % (2 * ny) == 0:
        ny *= 2
    nz = devices // ny

    def per_device(pend, pool, plan, lost, win, wout, gain):
        rows, hidden = pend.shape[1], pend.shape[2]
        width = hidden // devices
        cols = win.shape[3]
        slots = TICKS + 3
        win = jnp.transpose(win[0], (1, 0, 2))
        vmem = pl.BlockSpec(memory_space=pltpu.VMEM)
        smem = pl.BlockSpec(memory_space=pltpu.SMEM)
        hbm = pl.BlockSpec(memory_space=pl.ANY)
        bf = functools.partial(pltpu.VMEM, dtype=jnp.bfloat16)
        fl = functools.partial(pltpu.VMEM, dtype=jnp.float32)
        dma = pltpu.SemaphoreType.DMA
        return pl.pallas_call(
            functools.partial(relay_kernel, sections, nz, ny),
            out_shape=(
                jax.ShapeDtypeStruct((1, rows, hidden), jnp.bfloat16),
                jax.ShapeDtypeStruct((1, rows, width), jnp.bfloat16),
            ),
            in_specs=[smem, smem, hbm, hbm, hbm, hbm, vmem],
            out_specs=(hbm, hbm),
            scratch_shapes=[
                bf((3, hidden, cols)),
                bf((cols, hidden)),
                bf(pool.shape),
                bf((slots, devices, rows, width)),
                bf((slots, rows, width)),
                fl((rows, LANES)), fl((rows, LANES)), fl((rows, LANES)),
                fl((8, 3 * cols)),
                fl((rows, 3 * cols)),
                bf((rows, 3 * cols)),
                bf((rows, cols)),
                bf((ny - 1, nz, rows, width)),
                fl((nz, rows, width)),
                bf((3, ny - 1, nz, rows, width)),
                bf((nz - 1, rows, width)),
                bf((3, nz - 1, rows, width)),
                bf((slots, rows, width)),
                bf((rows, width)),
                bf((rows, width)),
                dma((devices,)), dma((devices,)), dma((2,)),
                dma((slots - 1,)), dma((slots - 1,)), dma((slots - 1, PIECES, nz)),
                dma((slots - 1,)), dma((slots - 1, PIECES, nz, ny - 1)),
                dma((1,)), dma((3, PIECES, nz - 1)), dma((1,)), dma((3, PIECES, ny - 1)),
                dma((1,)), dma((PIECES,)),
            ],
            compiler_params=pltpu.CompilerParams(
                collective_id=0, has_side_effects=True, vmem_limit_bytes=60 * 1024 * 1024
            ),
        )(lost, plan, pend, pool, win, wout[0], gain)

    placed = (
        P("section", None, None),
        P(None, None, "tp"),
        P(),
        P(),
        P("section", None, None, "tp"),
        P("section", "tp", None),
        P("section", None),
    )
    return jax.shard_map(
        per_device,
        mesh=mesh,
        in_specs=placed,
        out_specs=(P("section", None, None), P("section", None, "tp")),
        check_vma=False,
    )
```

time: 173 us -> 159 us (0.919)
  Pallas kernels: 168 us -> 153 us
    pallas_call x1, Pallas kernels: 168 us -> 153 us  [per_device(): pl.pallas_call(functools.partial(relay_kernel, sections, nz, ny), out_sha...]
where the time goes in v1:
time: 159 us; the launch traced here: 158 us
  Pallas kernels  153 us (96%)
  local copies, waits for them, and re-layouts  3.85 us (2%)
    pallas_call x1, Pallas kernels, per_device(): pl.pallas_call(functools.partial(relay_kernel, sections, nz, ny), out_sha...  153 us
    unnamed x2, local copies, waits for them, and re-layouts  3.85 us

profile of v1, /device:TPU:0, one launch (start us, length us, event | category | flops | bytes accessed | tf_op | source)
XLA Modules:
  0.0 158.3 jit_solution(15864760690940424287)
XLA Ops:
  1.3 153.1 %shard_map.86 = (bf16[1,128,4096]{2,1,0:T(8,128)(2,1)}, bf16[1,128,512]{2,1,0:T(8,128)(2,1)}) custom-call(s32[1]{0:T(128)S(6)} %copy.11.lost_ref, s32[4]{0:T(128)} %plan_ref.1, bf16[1,128,4096]{2,1,0:T(8,128)(2,1)} %pend_hbm.1, bf16[4,128,512]{2,1,0:T(8,128)(2,1)} %pool_hbm.1, bf16[3,4096,256]{2,1,0:T(8,128)(2,1)} %bitcast.4, bf16[256,4096]{1,0:T(8,128)(2,1)} %bitcast.5, ...), custom_call_target="tpu_custom_call" | custom-call | tf_op jit(solution)/shard_map/pallas_call | solution.py:516
  154.4 2.3 %copy.12 = bf16[1,128,4096]{2,1,0:T(8,128)(2,1)} copy(bf16[1,128,4096]{2,1,0:T(8,128)(2,1)} %get-tuple-element.4) | data formatting | bytes 2097152
  156.7 1.6 copy.13

commit v2 on v1

--- a/solution.py
+++ b/solution.py
@@ -22,7 +22,7 @@
     later_hbm, standby_hbm,
     win_ref, wout_ref, pool_buf, x_buf, y_buf, pivot, sum_1, sum_2, csum, acc, qkv, ctx,
     part, own_part, ry_buf, zs_buf, rz_buf, fwd_buf, spare_buf, spare_in,
-    w_sem, x_sem, io_sem, fw_s, ag_zs, ag_zr, ag_ys, ag_yr, rs_zs, rs_zr, rs_ys, rs_yr, sp_s, sp_r,
+    w_sem, x_sem, io_sem, fw_s, ag_zs, ag_zr, ag_ys, ag_yr, rs_zs, rs_zr, rs_ys, rs_yr, sp_s, sp_r, turn_sem,
 ):
     steps = TICKS + 2
     s = lax.axis_index("section")
@@ -105,6 +105,11 @@
 
     def small(n):
         return (n < s) if sections <= TICKS + 1 else (n < 0)
+
+    def follows(section, n):
+        return (section % 2 == 0) & (n > section) & needed(section, n) & needed(section + 1, n)
+
+    pools = list(enumerate(list(range(1, TICKS)) + [steps]))
 
     def when_full(n, h, body):
         if h == 0:
@@ -339,12 +344,16 @@
         for dz in far:
             for dy in range(1, ny):
                 part[dy - 1, dz] = partial_for(tp_at(dz, dy)).astype(jnp.bfloat16)
+        if sections <= TICKS + 1:
+            @pl.when(follows(s, n))
+            def _():
+                pl.semaphore_wait(turn_sem, 1)
+
         for h in range(PIECES):
             when_full(n, h, functools.partial(cross, h))
 
-        @pl.when((s == 0) & (n == 0))
-        def _():
-            pool_forward(1)
+        for tick, slot in pools:
+            pl.when((s == 0) & (n == tick))(functools.partial(pool_forward, slot))
 
         for dz in far:
             own_part[dz] = partial_for(tp_at(dz, 0))
@@ -392,6 +401,11 @@
             when_full(n, h, functools.partial(over_y, h))
             if h == PIECES - 2:
                 over_z(0)
+        if sections <= TICKS + 1:
+            @pl.when((s % 2 == 1) & follows(s - 1, n))
+            def _():
+                pl.semaphore_signal(turn_sem, inc=1, device_id={"section": prv, "tp": me}, device_id_type=MESH)
+
         for h in range(1, PIECES):
             when_full(n, h, functools.partial(over_z, h))
 
@@ -411,13 +425,11 @@
     def step(n, carry):
         @pl.when(needed(s, n))
         def _():
+            for tick, slot in pools:
+                pl.when((s == 0) & (n == tick))(functools.partial(pool_start, slot, tick))
+
             @pl.when(n == 0)
             def _():
-                @pl.when(s == 0)
-                def _():
-                    pool_copy.wait()
-                    pool_start(1, 0)
-
                 lax.fori_loop(0, devices, first_rows, 0)
                 wout_copy.wait()
 
@@ -428,19 +440,12 @@
             attend()
             project_out(n)
 
-            @pl.when((s == 0) & (n == 1))
-            def _():
-                pool_start(2, 1)
-                pool_forward(2)
-
         @pl.when(jnp.logical_not(needed(s, n)))
         def _():
             y_buf[n] = jnp.zeros((rows, width), jnp.bfloat16)
 
             @pl.when((s == 0) & (n == TICKS))
             def _():
-                pool_start(steps, TICKS - 1)
-                pool_forward(steps)
                 arrive_all(steps)
                 for j in range(devices):
                     later_copy(j).start()
@@ -459,9 +464,7 @@
 
         return carry
 
-    @pl.when(s > 0)
-    def _():
-        pool_copy.wait()
+    pool_copy.wait()
 
     lax.fori_loop(0, steps, step, 0)
 
@@ -544,7 +547,7 @@
                 dma((slots - 1,)), dma((slots - 1,)), dma((slots - 1, PIECES, nz)),
                 dma((slots - 1,)), dma((slots - 1, PIECES, nz, ny - 1)),
                 dma((1,)), dma((3, PIECES, nz - 1)), dma((1,)), dma((3, PIECES, ny - 1)),
-                dma((1,)), dma((PIECES,)),
+                dma((1,)), dma((PIECES,)), pltpu.SemaphoreType.REGULAR,
             ],
             compiler_params=pltpu.CompilerParams(
                 collective_id=0, has_side_effects=True, vmem_limit_bytes=60 * 1024 * 1024

time: 159 us -> 149 us (0.937)
  Pallas kernels: 153 us -> 144 us
    pallas_call x1, Pallas kernels: 153 us -> 144 us  [per_device(): pl.pallas_call(functools.partial(relay_kernel, sections, nz, ny), out_sha...]
where the time goes in v2:
time: 149 us
  Pallas kernels  144 us (97%)
  local copies, waits for them, and re-layouts  3.85 us (3%)
    pallas_call x1, Pallas kernels, per_device(): pl.pallas_call(functools.partial(relay_kernel, sections, nz, ny), out_sha...  144 us
    unnamed x2, local copies, waits for them, and re-layouts  3.85 us

profile of v2, /device:TPU:0, one launch (start us, length us, event | category | flops | bytes accessed | tf_op | source)
XLA Modules:
  0.0 148.7 jit_solution(6239945198522484942)
XLA Ops:
  1.3 143.6 %shard_map.86 = (bf16[1,128,4096]{2,1,0:T(8,128)(2,1)}, bf16[1,128,512]{2,1,0:T(8,128)(2,1)}) custom-call(s32[1]{0:T(128)S(6)} %copy.11.lost_ref, s32[4]{0:T(128)} %plan_ref.1, bf16[1,128,4096]{2,1,0:T(8,128)(2,1)} %pend_hbm.1, bf16[4,128,512]{2,1,0:T(8,128)(2,1)} %pool_hbm.1, bf16[3,4096,256]{2,1,0:T(8,128)(2,1)} %bitcast.4, bf16[256,4096]{1,0:T(8,128)(2,1)} %bitcast.5, ...), custom_call_target="tpu_custom_call" | custom-call | tf_op jit(solution)/shard_map/pallas_call | solution.py:519
  144.9 2.3 %copy.12 = bf16[1,128,4096]{2,1,0:T(8,128)(2,1)} copy(bf16[1,128,4096]{2,1,0:T(8,128)(2,1)} %get-tuple-element.4) | data formatting | bytes 2097152
  147.2 1.6 %copy.13 = bf16[1,128,512]{2,1,0:T(8,128)(2,1)} copy(bf16[1,128,512]{2,1,0:T(8,128)(2,1)} %get-tuple-element.5) | data formatting | bytes 262144

commit v3 on v2

--- a/solution.py
+++ b/solution.py
@@ -497,6 +497,22 @@
         standby_copy(h).wait()
 
 
+def hand_out(later_hbm, standby_hbm, later_out, standby_out, later_buf, standby_buf, in_sem, out_sem):
+    cut = later_buf.shape[1] // PIECES
+    parts = [(later_hbm.at[:, pl.ds(h * cut, cut)], later_buf.at[:, pl.ds(h * cut, cut)],
+              later_out.at[:, pl.ds(h * cut, cut)]) for h in range(PIECES)]
+    parts.append((standby_hbm, standby_buf, standby_out))
+    reads = [pltpu.make_async_copy(a, b, in_sem.at[k]) for k, (a, b, _) in enumerate(parts)]
+    writes = [pltpu.make_async_copy(b, c, out_sem.at[k]) for k, (_, b, c) in enumerate(parts)]
+    for copy in reads:
+        copy.start()
+    for read, write in zip(reads, writes):
+        read.wait()
+        write.start()
+    for copy in writes:
+        copy.wait()
+
+
 def solution(mesh):
     sections, devices = mesh.shape["section"], mesh.shape["tp"]
     ny = 1
@@ -516,7 +532,7 @@
         bf = functools.partial(pltpu.VMEM, dtype=jnp.bfloat16)
         fl = functools.partial(pltpu.VMEM, dtype=jnp.float32)
         dma = pltpu.SemaphoreType.DMA
-        return pl.pallas_call(
+        later, standby = pl.pallas_call(
             functools.partial(relay_kernel, sections, nz, ny),
             out_shape=(
                 jax.ShapeDtypeStruct((1, rows, hidden), jnp.bfloat16),
@@ -553,6 +569,16 @@
                 collective_id=0, has_side_effects=True, vmem_limit_bytes=60 * 1024 * 1024
             ),
         )(lost, plan, pend, pool, win, wout[0], gain)
+        return pl.pallas_call(
+            hand_out,
+            out_shape=(
+                jax.ShapeDtypeStruct(later.shape, later.dtype),
+                jax.ShapeDtypeStruct(standby.shape, standby.dtype),
+            ),
+            in_specs=[hbm, hbm],
+            out_specs=(hbm, hbm),
+            scratch_shapes=[bf(later.shape), bf(standby.shape), dma((PIECES + 1,)), dma((PIECES + 1,))],
+        )(later, standby)
 
     placed = (
         P("section", None, None),

time: 149 us -> 147 us (0.987)
  local copies, waits for them, and re-layouts: 3.85 us -> 0 us
  Pallas kernels: 144 us -> 146 us
    unnamed x2 -> x0, local copies, waits for them, and re-layouts: 3.85 us -> none
    pallas_call x0 -> x1, Pallas kernels: none -> 2.04 us  [per_device(): pl.pallas_call(hand_out, out_shape=(jax.ShapeDtypeStruct(later.shape, lat...]
where the time goes in v3:
time: 147 us
  Pallas kernels  146 us (99%)
    pallas_call x1, Pallas kernels, per_device(): pl.pallas_call(functools.partial(relay_kernel, sections, nz, ny), out_sha...  144 us

profile of v3, /device:TPU:0, one launch (start us, length us, event | category | flops | bytes accessed | tf_op | source)
XLA Modules:
  0.0 146.9 jit_solution(6020721714431123518)
XLA Ops:
  1.3 143.6 %shard_map.86 = (bf16[1,128,4096]{2,1,0:T(8,128)(2,1)}, bf16[1,128,512]{2,1,0:T(8,128)(2,1)}) custom-call(s32[1]{0:T(128)S(6)} %copy.9.lost_ref, s32[4]{0:T(128)} %plan_ref.1, bf16[1,128,4096]{2,1,0:T(8,128)(2,1)} %pend_hbm.1, bf16[4,128,512]{2,1,0:T(8,128)(2,1)} %pool_hbm.1, bf16[3,4096,256]{2,1,0:T(8,128)(2,1)} %bitcast.4, bf16[256,4096]{1,0:T(8,128)(2,1)} %bitcast.5, ...), custom_call_target="tpu_custom_call" | custom-call | tf_op jit(solution)/shard_map/pallas_call | solution.py:535
  144.9 2.0 %shard_map.87 = (bf16[1,128,4096]{2,1,0:T(8,128)(2,1)}, bf16[1,128,512]{2,1,0:T(8,128)(2,1)}) custom-call(bf16[1,128,4096]{2,1,0:T(8,128)(2,1)} %get-tuple-element.4.later_hbm, bf16[1,128,512]{2,1,0:T(8,128)(2,1)} %get-tuple-element.5.standby_hbm), custom_call_target="tpu_custom_call" | custom-call | tf_op jit(solution)/shard_map/pallas_call | solution.py:572
